TPU v7x, 32 devices: a whole 2x2x4 slice. The times are simulated.
32 devices in a mesh: ep: 8 (over z, x), tp: 4 (over y, core).
Axes of the slice: x: 2, y: 2, z: 4, core: 2. Of those that a mesh axis runs over, the one named last changes fastest.
Arguments:
- latents: float32 [2048, 2048], P('ep', 'tp'), may hold values from -6 to 6
- timesteps: int32 [3], replicated, may hold values from 50 to 650, as said below
- routes: int32 [2, 2048, 2], P(None, 'ep'), may hold values from 0 to 7, all different within a row; in each aligned block of 256 rows (0 to 255, 256 to 511, ..., all dimensions but the last counted through in order) at most 96 rows name the same one
- mod_weight: bfloat16 [2048, 3, 2048], P('ep', None, 'tp'), may hold values from -0.125 to 0.125
- router_weight: bfloat16 [2048, 8], replicated, may hold values from -0.125 to 0.125
- up_weight: bfloat16 [8, 2048, 8192], P('ep', None, 'tp'), may hold values from -0.125 to 0.125
- down_weight: bfloat16 [8, 8192, 2048], P('ep', 'tp'), may hold values from -0.0625 to 0.0625
Outputs:
- student_target: float32 [2048, 2048], P('ep', 'tp')
Inputs may be any that keep to these rules, and one draw needn't show every extreme that they name: timesteps fall by the same gap of 100 to 150 from each entry to the next; the first lies between 350 and 650. `routes`: the two experts of a token differ; among the 256 tokens of one index of ep in one substep, no expert is named more than 96 times, and in every substep some expert is named exactly 96 times by some index of ep.
All inputs are finite; a program needn't handle non-finite values.
Results may differ from a plain program's by a relative error of at most 0.013.
Values may be sent and summed in bfloat16 or wider, within the bound.
A program may use at most 64 MiB of HBM per device.

v0:
```python
import functools
import math

import jax
import jax.numpy as jnp
from jax import lax
from jax.experimental import pallas as pl
from jax.experimental.pallas import tpu as pltpu
from jax.sharding import PartitionSpec as P

MESH = pl.DeviceIdType.MESH
BF = jnp.bfloat16
F32 = jnp.float32


def plan(timestep):
    angle_value = (timestep.astype(jnp.float32) / 1000.0 + 0.008) / 1.008 * (math.pi / 2)
    return (jnp.cos(angle_value), jnp.sin(angle_value))


def embedding(timesteps_pair, width):
    half_width = width // 2
    frequency = jnp.exp(-math.log(10000.0) * jnp.arange(half_width, dtype=jnp.float32) / half_width)
    phases = timesteps_pair.astype(jnp.float32)[:, None] * frequency[None, :]
    return jnp.concatenate([jnp.cos(phases), jnp.sin(phases)], axis=1)


def xor_of(me, j, n):
    out, bit = 0, 1
    while bit < n:
        own = lax.rem(me // bit, 2)
        out = out + (lax.rem(own + 1, 2) if (j // bit) % 2 else own) * bit
        bit *= 2
    return out


def turned(rows):
    r, width = rows.shape
    if r < 128:
        rows = jnp.concatenate([rows, jnp.zeros((128 - r, width), F32)], axis=0)
    return rows.T


def kernel(
    n_ep, n_tp,
    scal, lat, modp, disp, pick, hots, rout, up_h, down_h,
    cur_o,
    up_v, down_v, mod_b, st_s, st_r, lg_s, lg_r, out_b, xb, hid, pas, par, y_s, y_r, own, ret_s, ret_r,
    wsem, mod_ss, mod_rs, st_ss, st_rs, lg_ss, lg_rs, aa_ss, aa_rs, ay_ss, ay_rs, sb_ss, sb_rs,
    pa_ss, pa_rs, ys_ss, ys_rs, re_ss, re_rs,
):
    me_e, me_t = lax.axis_index("ep"), lax.axis_index("tp")
    core, y = lax.rem(me_t, 2), me_t // 2
    n_y = n_tp // 2
    sib = (me_e, y * 2 + 1 - core)
    rows_t, width = lat.shape
    model = width * n_tp
    ff = hid.shape[1]
    cap = xb.shape[3]
    nb = y_s.shape[2]
    cb = n_ep // nb
    jg, bg = n_ep // 2, nb // 2
    group_rows = jg * cap
    nt = min(256, ff)
    pending = []

    up_c = pltpu.make_async_copy(up_h.at[0], up_v, wsem.at[0])
    down_c = pltpu.make_async_copy(down_h.at[0], down_v, wsem.at[1])
    up_c.start()
    down_c.start()

    def peer_e(j):
        half, pair = n_ep // 2, j // 2
        evens = (half + 1) // 2
        pair = 2 * pair if pair < evens else 2 * (pair - evens) + 1
        return (xor_of(me_e, 2 * pair + j % 2, n_ep), me_t)

    def peer_y(dy):
        return (me_e, lax.rem(y + dy, n_y) * 2 + core)

    def send(src, dst, ss, rs, to):
        copy = pltpu.make_async_remote_copy(
            src_ref=src, dst_ref=dst, send_sem=ss, recv_sem=rs, device_id=to, device_id_type=MESH
        )
        copy.start()
        pending.append(copy)

    def arrived(dst, ss, rs, to):
        pltpu.make_async_remote_copy(
            src_ref=dst, dst_ref=dst, send_sem=ss, recv_sem=rs, device_id=to, device_id_type=MESH
        ).wait_recv()

    barrier = pltpu.get_barrier_semaphore()
    for j in range(1, n_ep):
        pl.semaphore_signal(barrier, inc=1, device_id=peer_e(j), device_id_type=MESH)
    for dt in range(1, n_tp):
        pl.semaphore_signal(
            barrier, inc=1, device_id=(me_e, lax.rem(me_t + dt, n_tp)), device_id_type=MESH
        )
    pl.semaphore_wait(barrier, n_ep + n_tp - 2)

    def share(sub, src, dst, ss, rs):
        for dt in range(1, n_tp):
            send(
                src.at[sub], dst.at[sub, dt - 1], ss.at[sub, dt - 1], rs.at[sub, dt - 1],
                (me_e, lax.rem(me_t + dt, n_tp)),
            )

    def shared(sub, src, dst, ss, rs):
        total = src[sub]
        for dt in range(1, n_tp):
            arrived(
                dst.at[sub, dt - 1], ss.at[sub, dt - 1], rs.at[sub, dt - 1],
                (me_e, lax.rem(me_t + dt, n_tp)),
            )
            total = total + dst[sub, dt - 1]
        return total

    for j in range(1, n_ep):
        send(modp, mod_b.at[j - 1], mod_ss.at[j - 1], mod_rs.at[j - 1], peer_e(j))

    def slice_dot(t, store):
        sw = min(256, width)

        def body(n, carry):
            at = pl.ds(pl.multiple_of(t * width + n * sw, sw), sw)
            value = jnp.dot(hid[...], down_v[:, at], preferred_element_type=F32)
            store(pl.ds(pl.multiple_of(n * sw, sw), sw), value)
            return carry

        lax.fori_loop(0, width // sw, body, 0)

    modulation = None
    for sub in range(2):
        source = lat if sub == 0 else cur_o
        current = source[...]
        sums = jnp.sum(current, axis=1, keepdims=True)
        squares = jnp.sum(current * current, axis=1, keepdims=True)
        lane = lax.broadcasted_iota(jnp.int32, (rows_t, 128), 1)
        both = jnp.where(lane == 0, sums, jnp.where(lane == 1, squares, 0.0))
        st_s[sub] = both.T[0:8]
        share(sub, st_s, st_r, st_ss, st_rs)
        if sub == 0:
            modulation = modp[...]
            for j in range(1, n_ep):
                arrived(mod_b.at[j - 1], mod_ss.at[j - 1], mod_rs.at[j - 1], peer_e(j))
                modulation = modulation + mod_b[j - 1]
        stats = turned(shared(sub, st_s, st_r, st_ss, st_rs))
        row_mean = stats[:, 0:1] / model
        row_var = stats[:, 1:2] / model - row_mean * row_mean
        normed = (source[...] - row_mean) * lax.rsqrt(row_var + 1e-06)
        shift_row = modulation[3 * sub : 3 * sub + 1]
        scale_row = modulation[3 * sub + 1 : 3 * sub + 2]
        gate_row = modulation[3 * sub + 2 : 3 * sub + 3]
        modulated = (normed * (1.0 + scale_row) + shift_row).astype(BF)
        outgoing = jnp.dot(disp[sub], modulated, preferred_element_type=F32).astype(BF)
        out_b[sub] = outgoing.reshape(n_ep, cap, width)
        for j in range(1, n_ep):
            to = peer_e(j)
            send(out_b.at[sub, to[0]], xb.at[sub, me_t, j], aa_ss.at[sub, j], aa_rs.at[sub, j], to)
        xb[sub, me_t, 0] = out_b[sub, me_e]
        lg_s[sub] = lax.dot_general(
            rout[...], modulated, (((1,), (1,)), ((), ())), preferred_element_type=F32
        )
        share(sub, lg_s, lg_r, lg_ss, lg_rs)

        def gather_in(first, last):
            for b in range(first, last):
                js = pl.ds(b * cb, cb)
                for j in range(b * cb, b * cb + cb):
                    if j > 0:
                        arrived(xb.at[sub, me_t, j], aa_ss.at[sub, j], aa_rs.at[sub, j], peer_e(j))
                mine = xb.at[sub, me_t, js]
                for dy in range(1, n_y):
                    send(mine, mine, ay_ss.at[sub, dy, b], ay_rs.at[sub, dy, b], peer_y(dy))
                send(mine, mine, sb_ss.at[sub, 0, b], sb_rs.at[sub, 0, b], sib)

        def relay(first, last):
            for b in range(first, last):
                js = pl.ds(b * cb, cb)
                for dy in range(1, n_y):
                    came = xb.at[sub, lax.rem(y - dy + n_y, n_y) * 2 + core, js]
                    arrived(came, ay_ss.at[sub, dy, b], ay_rs.at[sub, dy, b], peer_y(dy))
                    send(came, came, sb_ss.at[sub, dy, b], sb_rs.at[sub, dy, b], sib)
            for b in range(first, last):
                js = pl.ds(b * cb, cb)
                for dy in range(n_y):
                    came = xb.at[sub, lax.rem(y - dy + n_y, n_y) * 2 + 1 - core, js]
                    arrived(came, sb_ss.at[sub, dy, b], sb_rs.at[sub, dy, b], sib)

        def first_gemm(g):
            def body(n, carry):
                at = pl.ds(pl.multiple_of(n * nt, nt), nt)
                total = None
                for t in range(n_tp):
                    rows = xb[sub, t, pl.ds(g * jg, jg)].reshape(group_rows, width)
                    term = jnp.dot(rows, up_v[pl.ds(t * width, width), at], preferred_element_type=F32)
                    total = term if total is None else total + term
                hid[:, at] = jax.nn.gelu(total).astype(BF)
                return carry

            lax.fori_loop(0, ff // nt, body, 0)

        def second_gemm(g):
            def for_sibling(dy):
                target = lax.rem(y + dy, n_y)

                def keep(at, value):
                    pas[sub, g, dy, :, at] = value.astype(BF)

                slice_dot(target * 2 + 1 - core, keep)
                send(
                    pas.at[sub, g, dy], par.at[sub, g, dy], pa_ss.at[sub, g, dy], pa_rs.at[sub, g, dy], sib
                )

            def from_sibling(dy):
                arrived(par.at[sub, g, dy], pa_ss.at[sub, g, dy], pa_rs.at[sub, g, dy], sib)

            for dy in range(1, n_y):
                for_sibling(dy)
            for dy in range(1, n_y):
                from_sibling(dy)

                def pass_on(at, value):
                    value = (value + par[sub, g, dy, :, at].astype(F32)).astype(BF)
                    y_s[sub, dy, pl.ds(g * bg, bg), :, at] = value.reshape(bg, cb * cap, value.shape[1])

                slice_dot(lax.rem(y + dy, n_y) * 2 + core, pass_on)
                for b in range(g * bg, g * bg + bg):
                    send(
                        y_s.at[sub, dy, b], y_r.at[sub, dy, b], ys_ss.at[sub, dy, b], ys_rs.at[sub, dy, b],
                        peer_y(dy),
                    )
            for_sibling(0)

            def hold(at, value):
                own[g, :, at] = value

            slice_dot(me_t, hold)
            from_sibling(0)

        def send_back(g):
            for b in range(g * bg, g * bg + bg):
                part = pl.ds((b - g * bg) * cb * cap, cb * cap)
                total = own[g, part, :] + par[sub, g, 0, part, :].astype(F32)
                for dy in range(1, n_y):
                    arrived(y_r.at[sub, dy, b], ys_ss.at[sub, dy, b], ys_rs.at[sub, dy, b], peer_y(dy))
                    total = total + y_r[sub, dy, b].astype(F32)
                ret_s[sub, pl.ds(b * cb, cb)] = total.astype(BF).reshape(cb, cap, width)
                for j in range(b * cb, b * cb + cb):
                    if j > 0:
                        send(
                            ret_s.at[sub, j], ret_r.at[sub, me_e], re_ss.at[sub, j], re_rs.at[sub, j], peer_e(j)
                        )
                    else:
                        ret_r[sub, me_e] = ret_s[sub, 0]

        gather_in(0, bg)
        relay(0, bg)
        if sub == 0:
            up_c.wait()
        first_gemm(0)
        gather_in(bg, nb)
        if sub == 0:
            down_c.wait()
        second_gemm(0)
        relay(bg, nb)
        first_gemm(1)
        send_back(0)
        second_gemm(1)
        logits = shared(sub, lg_s, lg_r, lg_ss, lg_rs)
        probs = [
            jax.nn.sigmoid(jnp.sum(hots[sub, k] * logits, axis=0, keepdims=True)) for k in range(2)
        ]
        both_p = probs[0] + probs[1]
        gates = turned(jnp.concatenate([probs[0] / both_p, probs[1] / both_p, jnp.zeros((6, rows_t), F32)], axis=0))
        send_back(1)
        for j in range(1, n_ep):
            to = peer_e(j)
            arrived(ret_r.at[sub, to[0]], re_ss.at[sub, j], re_rs.at[sub, j], to)
        returned = ret_r[sub].reshape(n_ep * cap, width)
        mix = gates[:, 0:1] * jnp.dot(pick[sub, 0], returned, preferred_element_type=F32)
        mix = mix + gates[:, 1:2] * jnp.dot(pick[sub, 1], returned, preferred_element_type=F32)
        now = source[...]
        noise = now + gate_row * mix
        clean = (now - scal[4 * sub + 1] * noise) * scal[4 * sub]
        cur_o[...] = scal[4 * sub + 2] * clean + scal[4 * sub + 3] * noise
    for copy in pending:
        copy.wait_send()


def per_device(n_ep, n_tp, latents, timesteps, routes, mod_weight, router_weight, up_weight, down_weight):
    tok_rows, width = latents.shape
    model, experts = router_weight.shape
    capacity = 3 * tok_rows // experts
    cap = -(-capacity // 16) * 16
    ff = up_weight.shape[2]
    mod_rows = mod_weight.shape[0]
    condition = embedding(timesteps[:2], model).astype(BF)
    cond_rows = lax.dynamic_slice_in_dim(condition, lax.axis_index("ep") * mod_rows, mod_rows, 1)
    mod_part = jnp.einsum("sd,dkf->skf", cond_rows, mod_weight, preferred_element_type=F32)
    mod_part = jnp.concatenate([mod_part.reshape(6, width), jnp.zeros((2, width), F32)], axis=0)
    rout = lax.dynamic_slice_in_dim(router_weight, lax.axis_index("tp") * width, width, 0).T
    ids = jnp.arange(experts, dtype=jnp.int32)
    flat_hot = (routes.reshape(2, 2 * tok_rows)[:, :, None] == ids).astype(jnp.int32)
    before = jnp.cumsum(flat_hot, axis=1) - flat_hot
    slot = jnp.sum(before * flat_hot, axis=2)
    dest = (routes.reshape(2, 2 * tok_rows) * cap + slot).reshape(2, tok_rows, 2)
    slots = jnp.arange(experts * cap, dtype=jnp.int32)
    disp = jnp.any(dest[:, None] == slots[None, :, None, None], axis=3).astype(BF)
    pick = (jnp.swapaxes(dest, 1, 2)[..., None] == slots).astype(BF)
    hots = (jnp.swapaxes(routes, 1, 2)[:, :, None, :] == ids[None, None, :, None]).astype(F32)
    marks = [plan(timesteps[i]) for i in range(3)]
    scal = jnp.stack(
        [v for s in range(2) for v in (1.0 / marks[s][0], marks[s][1], marks[s + 1][0], marks[s + 1][1])]
    )
    n_y = n_tp // 2
    nb = min(8, n_ep)
    cb = n_ep // nb
    group_rows = n_ep // 2 * cap
    vm = pltpu.VMEM
    dma = pltpu.SemaphoreType.DMA
    scratch = [
        vm((model, ff), BF),
        vm((ff, model), BF),
        vm((n_ep - 1, 8, width), F32),
        vm((2, 8, tok_rows), F32),
        vm((2, n_tp - 1, 8, tok_rows), F32),
        vm((2, experts, tok_rows), F32),
        vm((2, n_tp - 1, experts, tok_rows), F32),
        vm((2, n_ep, cap, width), BF),
        vm((2, n_tp, n_ep, cap, width), BF),
        vm((group_rows, ff), BF),
        vm((2, 2, n_y, group_rows, width), BF),
        vm((2, 2, n_y, group_rows, width), BF),
        vm((2, n_y, nb, cb * cap, width), BF),
        vm((2, n_y, nb, cb * cap, width), BF),
        vm((2, group_rows, width), F32),
        vm((2, n_ep, cap, width), BF),
        vm((2, n_ep, cap, width), BF),
        dma((2,)),
        dma((n_ep - 1,)), dma((n_ep - 1,)),
        dma((2, n_tp - 1)), dma((2, n_tp - 1)),
        dma((2, n_tp - 1)), dma((2, n_tp - 1)),
        dma((2, n_ep)), dma((2, n_ep)),
        dma((2, n_y, nb)), dma((2, n_y, nb)),
        dma((2, n_y, nb)), dma((2, n_y, nb)),
        dma((2, 2, n_y)), dma((2, 2, n_y)),
        dma((2, n_y, nb)), dma((2, n_y, nb)),
        dma((2, n_ep)), dma((2, n_ep)),
    ]
    in_vmem = pl.BlockSpec(memory_space=pltpu.VMEM)
    current = pl.pallas_call(
        functools.partial(kernel, n_ep, n_tp),
        out_shape=jax.ShapeDtypeStruct((tok_rows, width), F32),
        in_specs=[pl.BlockSpec(memory_space=pltpu.SMEM)]
        + [in_vmem] * 6
        + [pl.BlockSpec(memory_space=pl.ANY)] * 2,
        out_specs=in_vmem,
        scratch_shapes=scratch,
        compiler_params=pltpu.CompilerParams(
            collective_id=0, has_side_effects=True, vmem_limit_bytes=60 * 1024 * 1024
        ),
    )(scal, latents, mod_part, disp, pick, hots, rout, up_weight, down_weight)
    ratio = marks[2][1] / marks[0][1]
    return (current - ratio * latents) / (marks[2][0] - ratio * marks[0][0])


def solution(mesh):
    in_specs = (
        P("ep", "tp"),
        P(),
        P(None, "ep", None),
        P("ep", None, "tp"),
        P(),
        P("ep", None, "tp"),
        P("ep", "tp", None),
    )
    body = functools.partial(per_device, mesh.shape["ep"], mesh.shape["tp"])
    return jax.shard_map(body, mesh=mesh, in_specs=in_specs, out_specs=P("ep", "tp"), check_vma=False)
```

profile of v0, /device:TPU:0, one launch (start us, length us, event | category | flops | bytes accessed | tf_op | source)
XLA Modules:
  0.0 161.3 jit_solution(15779923925644102204)
XLA Ops:
  0.0 0.0 copy-start
  0.0 0.7 slice_convert_fusion
  0.7 1.4 fusion.14
  4.7 0.6 stack.32.scal
  5.3 0.2 fusion.7
  5.5 0.0 copy-done
  5.5 0.2 fusion.9
  5.7 0.6 concatenate.8.modp
  6.4 1.3 dynamic-slice_bitcast_fusion.rout
  7.6 1.3 fusion.5.hots
  8.9 0.8 copy.24
  9.8 0.2 eq.68
  10.0 0.2 eq.64
  10.1 2.3 %reduce-window.6 = s32[2,8,4,128]{3,1,2,0:T(8,128)S(1)} reduce-window(s32[2,8,4,128]{3,1,2,0:T(8,128)S(1)} %fusion.4, s32[]{:T(128)} %constant.49.clone.1), window={size=1x1x1x128 pad=0_0x0_0x0_0x127_0}, to_apply=%region_0.0 | reduce-window | flops 1040384 | bytes 65540 | tf_op jit(solution)/shard_map/reduce-window
  12.4 0.3 slice_reduce_fusion
  12.7 0.1 fusion.3
  12.9 0.2 reduce_sum.12
  13.1 0.1 copy.26
  13.2 0.7 multiply_add_fusion
  13.9 0.7 fusion
  14.6 1.0 convert_element_type.38.disp
  15.6 1.5 fusion.1.pick
  17.1 0.0 copy-start.1
  17.1 142.3 %shard_map.73 = f32[256,512]{1,0:T(8,128)} custom-call(f32[8]{0:T(128)} %stack.32.scal, f32[256,512]{1,0:T(8,128)} %lat.1, f32[8,512]{1,0:T(8,128)} %concatenate.8.modp, bf16[2,768,256]{2,1,0:T(8,128)(2,1)} %convert_element_type.38.disp, bf16[2,2,256,768]{3,2,1,0:T(8,128)(2,1)} %fusion.1.pick, f32[2,2,8,256]{3,2,1,0:T(8,128)} %fusion.5.hots, ...), custom_call_target="tpu_custom_call" | custom-call | tf_op jit(solution)/shard_map/pallas_call | solution.py:353
  159.4 0.0 copy-done.1
  159.4 1.9 %subtract_divide_fusion = f32[256,512]{1,0:T(8,128)} fusion(f32[256,512]{1,0:T(8,128)} %shard_map.73, f32[256,512]{1,0:T(8,128)S(1)} %copy-done.1, f32[]{:T(128)S(6)} %sub.11, f32[]{:T(128)} %bitcast.8), kind=kLoop, calls=%fused_computation.4 | loop fusion | flops 393216 | bytes 1572872 | tf_op jit(solution)/shard_map/div | solution.py:366
  (6 shorter events, 0.1 us)
Async XLA Ops:
  0.0 5.5 %copy-start = (bf16[256,3,512]{2,0,1:T(8,128)(2,1)S(1)}, bf16[256,3,512]{2,0,1:T(8,128)(2,1)}, u32[]{:S(2)}) copy-start(bf16[256,3,512]{2,0,1:T(8,128)(2,1)} %param.10) | copy-start | bytes 2359300
  17.1 142.3 %copy-start.1 = (f32[256,512]{1,0:T(8,128)S(1)}, f32[256,512]{1,0:T(8,128)}, u32[]{:S(2)}) copy-start(f32[256,512]{1,0:T(8,128)} %lat.1) | copy-start | bytes 1572868
where the time goes:
time: 162 us; the launch traced here: 161 us
  Pallas kernels  142 us (88%)
  other arithmetic  10.5 us (6%)
  local copies, waits for them, and re-layouts  5.76 us (4%)
  between operations  2.57 us (2%)
    pallas_call x1, Pallas kernels, per_device(): pl.pallas_call(functools.partial(kernel, n_ep, n_tp), out_shape=jax.Shape...  142 us

commit v1 on v0

v1 whole, which is shorter than its diff:
```python
import functools
import math

import jax
import jax.numpy as jnp
from jax import lax
from jax.experimental import pallas as pl
from jax.experimental.pallas import tpu as pltpu
from jax.sharding import PartitionSpec as P

MESH = pl.DeviceIdType.MESH
BF = jnp.bfloat16
F32 = jnp.float32
GROUPS = 4


def xor_of(me, j, n):
    out, bit = 0, 1
    while bit < n:
        own = lax.rem(me // bit, 2)
        out = out + (1 - own if (j // bit) % 2 else own) * bit
        bit *= 2
    return out


def turned(rows):
    r, width = rows.shape
    if r < 128:
        rows = jnp.concatenate([rows, jnp.zeros((128 - r, width), F32)], axis=0)
    return rows.T


def process_order(n_ep):
    return list(range(n_ep))


def send_order(n_ep):
    return list(range(n_ep))


SCHEDULE = (
    "A0", "A1", "A2", "A3", "R0", "R1", "L", "W0", "W1", "F0", "A4", "R2", "G0.0", "A5", "R3", "G0.1", "G0.2",
    "A6", "R4", "G0.3", "W2", "W3", "F1", "A7", "R5", "G1.0", "R6", "G1.1", "G1.2", "R7", "G1.3", "W4", "W5",
    "F2", "S0", "S1", "G2.0", "G2.1", "G2.2", "G2.3", "W6", "W7", "F3", "S2", "S3", "M0", "M1", "G3.0",
    "G3.1", "G3.2", "G3.3", "S4", "S5", "M2", "M3", "S6", "S7", "M4", "M5", "M6", "M7",
)


def kernel(
    n_ep, n_tp,
    ts, lat_h, mod_h, rt_h, rw_h, up_h, down_h,
    out,
    up_v, down_v, lat_v, cur_v, mod_v, rt_v, rw_v,
    ma_s, ma_r, mb_s, mb_r, modv, st_s, st_r, lg_s, lg_r,
    mdl, disp_v, pick_v, gate_v, mix_v,
    out_b, xb, hid, pas, par, y_s, y_r, own, ret_s, ret_r,
    wsem, ma_ss, ma_rs, mb_ss, mb_rs, st_ss, st_rs, lg_ss, lg_rs, aa_ss, aa_rs, ay_ss, ay_rs, sb_ss, sb_rs,
    pa_ss, pa_rs, ys_ss, ys_rs, re_ss, re_rs,
):
    me_e, me_t = lax.axis_index("ep"), lax.axis_index("tp")
    core, y = lax.rem(me_t, 2), me_t // 2
    n_y = n_tp // 2
    sib = (me_e, y * 2 + 1 - core)
    rows_t, width = lat_v.shape
    model = width * n_tp
    ff = hid.shape[1]
    cap = xb.shape[3]
    nb = y_s.shape[2]
    cb = n_ep // nb
    jg, bg = n_ep // GROUPS, nb // GROUPS
    group_rows = jg * cap
    nt = min(1024, ff)
    order = process_order(n_ep)
    place = {mask: j for j, mask in enumerate(order)}

    def local(src, dst, i):
        copy = pltpu.make_async_copy(src, dst, wsem.at[i])
        copy.start()
        return copy

    lat_c = local(lat_h, lat_v, 0)
    mod_c = local(mod_h, mod_v, 1)
    rt_c = local(rt_h, rt_v, 2)
    rw_c = local(rw_h.at[:, pl.ds(pl.multiple_of(me_t * width, width), width)], rw_v, 3)
    up_c = local(up_h.at[0], up_v, 4)
    down_c = local(down_h.at[0], down_v, 5)

    def peer_m(mask):
        return (xor_of(me_e, mask, n_ep), me_t)

    def peer_e(j):
        return peer_m(order[j])

    def peer_y(dy):
        return (me_e, lax.rem(y + dy, n_y) * 2 + core)

    def peer_t(dt):
        return (me_e, lax.rem(me_t + dt, n_tp))

    barrier = pltpu.get_barrier_semaphore()
    for j in range(1, n_ep):
        pl.semaphore_signal(barrier, inc=1, device_id=peer_m(j), device_id_type=MESH)
    for dt in range(1, n_tp):
        pl.semaphore_signal(barrier, inc=1, device_id=peer_t(dt), device_id_type=MESH)

    def remote(src, dst, ss, rs, to):
        return pltpu.make_async_remote_copy(
            src_ref=src, dst_ref=dst, send_sem=ss, recv_sem=rs, device_id=to, device_id_type=MESH
        )

    once = []

    def arrived(dst, ss, rs, to):
        remote(dst, dst, ss, rs, to).wait_recv()

    half = model // 2
    mod_rows = mod_v.shape[1]
    times = [ts[i].astype(F32) for i in range(3)]
    row = lax.broadcasted_iota(jnp.int32, (8, 128), 0)
    tcol = jnp.where(row == 0, times[0], jnp.where(row == 1, times[1], times[2]))
    angle = (tcol / 1000.0 + 0.008) / 1.008 * (math.pi / 2)
    cosv, sinv = jnp.cos(angle), jnp.sin(angle)
    cos_t = [cosv[i : i + 1, 0:1] for i in range(3)]
    sin_t = [sinv[i : i + 1, 0:1] for i in range(3)]
    first = lax.rem(me_e * mod_rows, half)
    feature = (lax.broadcasted_iota(jnp.int32, (8, mod_rows), 1) + first).astype(F32)
    frequency = jnp.exp(-math.log(10000.0) * feature / half)
    row = lax.broadcasted_iota(jnp.int32, (8, mod_rows), 0)
    phase = jnp.where(row == 0, times[0], times[1]) * frequency
    condition = jnp.where(me_e * mod_rows >= half, jnp.sin(phase), jnp.cos(phase)).astype(BF)
    mod_c.wait()
    parts = [jnp.dot(condition, mod_v[c], preferred_element_type=F32) for c in range(3)]
    ma_s[...] = jnp.concatenate([parts[0][0:1], parts[1][0:1]], axis=0)
    mb_s[...] = jnp.concatenate([parts[2][0:1], parts[0][1:2], parts[1][1:2], parts[2][1:2]], axis=0)
    rt_c.wait()
    rw_c.wait()
    lat_c.wait()
    cur_v[...] = lat_v[...]
    pl.semaphore_wait(barrier, n_ep + n_tp - 2)

    def share_one(src, dst, ss, rs):
        for j in range(1, n_ep):
            copy = remote(src, dst.at[j - 1], ss.at[j - 1], rs.at[j - 1], peer_m(j))
            copy.start()
            once.append(copy)

    def summed(src, dst, ss, rs):
        total = src[...]
        for j in range(1, n_ep):
            arrived(dst.at[j - 1], ss.at[j - 1], rs.at[j - 1], peer_m(j))
            total = total + dst[j - 1]
        return total

    share_one(ma_s, ma_r, ma_ss, ma_rs)
    share_one(mb_s, mb_r, mb_ss, mb_rs)

    sent = []

    def substep(sub, carry):
        pending = []

        def send(src, dst, ss, rs, to):
            copy = remote(src, dst, ss, rs, to)
            copy.start()
            pending.append(copy)

        def share(src, dst, ss, rs):
            for dt in range(1, n_tp):
                send(src.at[sub], dst.at[sub, dt - 1], ss.at[sub, dt - 1], rs.at[sub, dt - 1], peer_t(dt))

        def shared(src, dst, ss, rs):
            total = src[sub]
            for dt in range(1, n_tp):
                arrived(dst.at[sub, dt - 1], ss.at[sub, dt - 1], rs.at[sub, dt - 1], peer_t(dt))
                total = total + dst[sub, dt - 1]
            return total

        current = cur_v[...]
        sums = jnp.sum(current, axis=1, keepdims=True)
        squares = jnp.sum(current * current, axis=1, keepdims=True)
        lane = lax.broadcasted_iota(jnp.int32, (rows_t, 128), 1)
        both = jnp.where(lane == 0, sums, jnp.where(lane == 1, squares, 0.0))
        st_s[sub] = both.T[0:8]
        share(st_s, st_r, st_ss, st_rs)

        spot = lax.broadcasted_iota(jnp.int32, (n_ep, rows_t), 0)
        experts = jnp.zeros((n_ep, rows_t), jnp.int32)
        for j in range(n_ep):
            experts = jnp.where(spot == j, xor_of(me_e, order[j], n_ep), experts)
        routes = [rt_v[sub, k : k + 1, :] for k in range(2)]
        hot = [routes[k] == experts for k in range(2)]
        either = jnp.where(hot[0], 1.0, jnp.where(hot[1], 1.0, 0.0))
        earlier = lax.broadcasted_iota(jnp.int32, (rows_t, rows_t), 0) < lax.broadcasted_iota(
            jnp.int32, (rows_t, rows_t), 1
        )
        earlier = jnp.where(earlier, 1.0, 0.0).astype(BF)
        slot = jnp.dot(either.astype(BF), earlier, preferred_element_type=F32)
        slot = jnp.where(either > 0.5, slot, -1.0)
        ranks = lax.broadcasted_iota(jnp.int32, (cap, rows_t), 0).astype(F32)
        for j in range(n_ep):
            disp_v[j] = jnp.where(slot[j : j + 1] == ranks, 1.0, 0.0).astype(BF)
        slot_t = turned(slot)
        ranks = lax.broadcasted_iota(jnp.int32, (rows_t, cap), 1).astype(F32)
        for j in range(n_ep):
            pick_v[j] = jnp.where(slot_t[:, j : j + 1] == ranks, 1.0, 0.0).astype(BF)

        @pl.when(sub == 0)
        def _():
            total = summed(ma_s, ma_r, ma_ss, ma_rs)
            modv[0, 0:2] = total

        stats = turned(shared(st_s, st_r, st_ss, st_rs))
        row_mean = stats[:, 0:1] / model
        row_var = stats[:, 1:2] / model - row_mean * row_mean
        normed = (cur_v[...] - row_mean) * lax.rsqrt(row_var + 1e-06)
        mdl[...] = (normed * (1.0 + modv[sub, 1:2]) + modv[sub, 0:1]).astype(BF)
        for mask in send_order(n_ep):
            j = place[mask]
            outgoing = jnp.dot(disp_v[j], mdl[...], preferred_element_type=F32).astype(BF)
            if mask == 0:
                xb[sub, me_t, j] = outgoing
            else:
                out_b[sub, j] = outgoing
                send(out_b.at[sub, j], xb.at[sub, me_t, j], aa_ss.at[sub, j], aa_rs.at[sub, j], peer_e(j))
        lg_s[sub] = lax.dot_general(rw_v[...], mdl[...], (((1,), (1,)), ((), ())), preferred_element_type=F32)
        share(lg_s, lg_r, lg_ss, lg_rs)
        mix_v[...] = jnp.zeros((rows_t, width), F32)

        def step_a(b):
            js = pl.ds(b * cb, cb)
            for j in range(b * cb, b * cb + cb):
                if order[j] > 0:
                    arrived(xb.at[sub, me_t, j], aa_ss.at[sub, j], aa_rs.at[sub, j], peer_e(j))
            mine = xb.at[sub, me_t, js]
            for dy in range(1, n_y):
                send(mine, mine, ay_ss.at[sub, dy, b], ay_rs.at[sub, dy, b], peer_y(dy))
            send(mine, mine, sb_ss.at[sub, 0, b], sb_rs.at[sub, 0, b], sib)

        def step_r(b):
            js = pl.ds(b * cb, cb)
            for dy in range(1, n_y):
                came = xb.at[sub, lax.rem(y - dy + n_y, n_y) * 2 + core, js]
                arrived(came, ay_ss.at[sub, dy, b], ay_rs.at[sub, dy, b], peer_y(dy))
                send(came, came, sb_ss.at[sub, dy, b], sb_rs.at[sub, dy, b], sib)

        def step_w(b):
            js = pl.ds(b * cb, cb)
            for dy in range(n_y):
                came = xb.at[sub, lax.rem(y - dy + n_y, n_y) * 2 + 1 - core, js]
                arrived(came, sb_ss.at[sub, dy, b], sb_rs.at[sub, dy, b], sib)

        def step_l():
            logits = shared(lg_s, lg_r, lg_ss, lg_rs)
            ids = lax.broadcasted_iota(jnp.int32, (n_ep, rows_t), 0)
            probs = [
                jax.nn.sigmoid(jnp.sum(jnp.where(routes[k] == ids, logits, 0.0), axis=0, keepdims=True))
                for k in range(2)
            ]
            both_p = probs[0] + probs[1]
            gates = jnp.where(hot[0], probs[0] / both_p, jnp.where(hot[1], probs[1] / both_p, 0.0))
            gate_v[...] = turned(gates)

        def first_gemm(g):
            if g == 0:

                @pl.when(sub == 0)
                def _():
                    up_c.wait()

            def body(n, carry):
                at = pl.ds(pl.multiple_of(n * nt, nt), nt)
                total = None
                for t in range(n_tp):
                    rows = xb[sub, t, pl.ds(g * jg, jg)].reshape(group_rows, width)
                    term = jnp.dot(rows, up_v[pl.ds(t * width, width), at], preferred_element_type=F32)
                    total = term if total is None else total + term
                hid[:, at] = jax.nn.gelu(total).astype(BF)
                return carry

            lax.fori_loop(0, ff // nt, body, 0)

        def slice_dot(t, store):
            sw = min(512, width)

            def body(n, carry):
                at = pl.ds(pl.multiple_of(t * width + n * sw, sw), sw)
                value = jnp.dot(hid[...], down_v[:, at], preferred_element_type=F32)
                store(pl.ds(pl.multiple_of(n * sw, sw), sw), value)
                return carry

            lax.fori_loop(0, width // sw, body, 0)

        def for_sibling(g, dy):
            target = lax.rem(y + dy, n_y)

            def keep(at, value):
                pas[sub, g, dy, :, at] = value.astype(BF)

            slice_dot(target * 2 + 1 - core, keep)
            send(pas.at[sub, g, dy], par.at[sub, g, dy], pa_ss.at[sub, g, dy], pa_rs.at[sub, g, dy], sib)

        def from_sibling(g, dy):
            arrived(par.at[sub, g, dy], pa_ss.at[sub, g, dy], pa_rs.at[sub, g, dy], sib)

        def second_gemm(g, part):
            if g == 0 and part == 0:

                @pl.when(sub == 0)
                def _():
                    down_c.wait()

            if part == 0:
                for dy in range(1, n_y):
                    for_sibling(g, dy)
            elif part == 1:
                for_sibling(g, 0)
            elif part == 2:
                for dy in range(1, n_y):
                    from_sibling(g, dy)

                    def pass_on(at, value):
                        value = (value + par[sub, g, dy, :, at].astype(F32)).astype(BF)
                        y_s[sub, dy, pl.ds(g * bg, bg), :, at] = value.reshape(bg, cb * cap, value.shape[1])

                    slice_dot(lax.rem(y + dy, n_y) * 2 + core, pass_on)
                    for b in range(g * bg, g * bg + bg):
                        send(
                            y_s.at[sub, dy, b], y_r.at[sub, dy, b], ys_ss.at[sub, dy, b], ys_rs.at[sub, dy, b],
                            peer_y(dy),
                        )
            else:

                def hold(at, value):
                    own[g, :, at] = value

                slice_dot(me_t, hold)
                from_sibling(g, 0)

        def send_back(b):
            g = b // bg
            part = pl.ds((b - g * bg) * cb * cap, cb * cap)
            total = own[g, part, :] + par[sub, g, 0, part, :].astype(F32)
            for dy in range(1, n_y):
                arrived(y_r.at[sub, dy, b], ys_ss.at[sub, dy, b], ys_rs.at[sub, dy, b], peer_y(dy))
                total = total + y_r[sub, dy, b].astype(F32)
            ret_s[sub, pl.ds(b * cb, cb)] = total.astype(BF).reshape(cb, cap, width)
            for j in range(b * cb, b * cb + cb):
                if order[j] > 0:
                    send(ret_s.at[sub, j], ret_r.at[sub, j], re_ss.at[sub, j], re_rs.at[sub, j], peer_e(j))

        def mix_in(b):
            for j in range(b * cb, b * cb + cb):
                if order[j] > 0:
                    arrived(ret_r.at[sub, j], re_ss.at[sub, j], re_rs.at[sub, j], peer_e(j))
                    came = ret_r[sub, j]
                else:
                    came = ret_s[sub, j]
                mix_v[...] += gate_v[:, j : j + 1] * jnp.dot(pick_v[j], came, preferred_element_type=F32)

        steps = dict(A=step_a, R=step_r, W=step_w, F=first_gemm, S=send_back, M=mix_in)
        for word in SCHEDULE:
            if word == "L":
                step_l()
            elif word[0] == "G":
                g, part = word[1:].split(".")
                second_gemm(int(g), int(part))
            else:
                steps[word[0]](int(word[1:]))

        @pl.when(sub == 0)
        def _():
            total = summed(mb_s, mb_r, mb_ss, mb_rs)
            modv[0, 2:3] = total[0:1]
            modv[1, 0:3] = total[1:4]

        now = cur_v[...]
        noise = now + modv[sub, 2:3] * mix_v[...]
        first_sub = sub == 0
        cos_now, sin_now, cos_next, sin_next = [
            jnp.where(first_sub, a, b)
            for a, b in (
                (cos_t[0], cos_t[1]), (sin_t[0], sin_t[1]), (cos_t[1], cos_t[2]), (sin_t[1], sin_t[2])
            )
        ]
        clean = (now - sin_now * noise) * (1.0 / cos_now)
        cur_v[...] = cos_next * clean + sin_next * noise
        sent.extend(pending)
        for copy in pending:
            copy.wait_send()
        return carry

    lax.fori_loop(0, 2, substep, 0)
    ratio = sin_t[2] / sin_t[0]
    scale = 1.0 / (cos_t[2] - ratio * cos_t[0])
    out[...] = (cur_v[...] - ratio * lat_v[...]) * scale
    for copy in once:
        copy.wait_send()


def per_device(n_ep, n_tp, latents, timesteps, routes, mod_weight, router_weight, up_weight, down_weight):
    tok_rows, width = latents.shape
    model, experts = router_weight.shape
    capacity = 3 * tok_rows // experts
    cap = -(-capacity // 16) * 16
    ff = up_weight.shape[2]
    mod_rows = mod_weight.shape[0]
    n_y = n_tp // 2
    nb = min(8, n_ep)
    cb = n_ep // nb
    group_rows = n_ep // GROUPS * cap
    vm = pltpu.VMEM
    dma = pltpu.SemaphoreType.DMA
    scratch = [
        vm((model, ff), BF),
        vm((ff, model), BF),
        vm((tok_rows, width), F32),
        vm((tok_rows, width), F32),
        vm((3, mod_rows, width), BF),
        vm((2, 2, tok_rows), jnp.int32),
        vm((experts, width), BF),
        vm((2, width), F32),
        vm((n_ep - 1, 2, width), F32),
        vm((4, width), F32),
        vm((n_ep - 1, 4, width), F32),
        vm((2, 8, width), F32),
        vm((2, 8, tok_rows), F32),
        vm((2, n_tp - 1, 8, tok_rows), F32),
        vm((2, experts, tok_rows), F32),
        vm((2, n_tp - 1, experts, tok_rows), F32),
        vm((tok_rows, width), BF),
        vm((n_ep, cap, tok_rows), BF),
        vm((n_ep, tok_rows, cap), BF),
        vm((tok_rows, 128), F32),
        vm((tok_rows, width), F32),
        vm((2, n_ep, cap, width), BF),
        vm((2, n_tp, n_ep, cap, width), BF),
        vm((group_rows, ff), BF),
        vm((2, GROUPS, n_y, group_rows, width), BF),
        vm((2, GROUPS, n_y, group_rows, width), BF),
        vm((2, n_y, nb, cb * cap, width), BF),
        vm((2, n_y, nb, cb * cap, width), BF),
        vm((GROUPS, group_rows, width), F32),
        vm((2, n_ep, cap, width), BF),
        vm((2, n_ep, cap, width), BF),
        dma((6,)),
        dma((n_ep - 1,)), dma((n_ep - 1,)),
        dma((n_ep - 1,)), dma((n_ep - 1,)),
        dma((2, n_tp - 1)), dma((2, n_tp - 1)),
        dma((2, n_tp - 1)), dma((2, n_tp - 1)),
        dma((2, n_ep)), dma((2, n_ep)),
        dma((2, n_y, nb)), dma((2, n_y, nb)),
        dma((2, n_y, nb)), dma((2, n_y, nb)),
        dma((2, GROUPS, n_y)), dma((2, GROUPS, n_y)),
        dma((2, n_y, nb)), dma((2, n_y, nb)),
        dma((2, n_ep)), dma((2, n_ep)),
    ]
    return pl.pallas_call(
        functools.partial(kernel, n_ep, n_tp),
        out_shape=jax.ShapeDtypeStruct((tok_rows, width), F32),
        in_specs=[pl.BlockSpec(memory_space=pltpu.SMEM)] + [pl.BlockSpec(memory_space=pltpu.HBM)] * 6,
        out_specs=pl.BlockSpec(memory_space=pltpu.VMEM),
        scratch_shapes=scratch,
        compiler_params=pltpu.CompilerParams(
            collective_id=0, has_side_effects=True, vmem_limit_bytes=60 * 1024 * 1024
        ),
    )(
        timesteps, latents, jnp.swapaxes(mod_weight, 0, 1), jnp.swapaxes(routes, 1, 2), router_weight.T,
        up_weight, down_weight,
    )


def solution(mesh):
    in_specs = (
        P("ep", "tp"),
        P(),
        P(None, "ep", None),
        P("ep", None, "tp"),
        P(),
        P("ep", None, "tp"),
        P("ep", "tp", None),
    )
    body = functools.partial(per_device, mesh.shape["ep"], mesh.shape["tp"])
    return jax.shard_map(body, mesh=mesh, in_specs=in_specs, out_specs=P("ep", "tp"), check_vma=False)
```

time: 162 us -> 137 us (0.85)
  the two profiles are of different devices: /device:TPU:0 before, /device:TPU:17 now
where the time goes in v1:
time: 137 us
  Pallas kernels  135 us (99%)
  local copies, waits for them, and re-layouts  1.87 us (1%)
    pallas_call x1, Pallas kernels, per_device(): pl.pallas_call(functools.partial(kernel, n_ep, n_tp), out_shape=jax.Shape...  135 us

profile of v1, /device:TPU:17, one launch (start us, length us, event | category | flops | bytes accessed | tf_op | source)
XLA Modules:
  0.0 136.6 jit_solution(9209021966270487568)
XLA Ops:
  0.0 134.7 %shard_map.73 = f32[256,512]{1,0:T(8,128)} custom-call(s32[3]{0:T(128)} %ts.1, f32[256,512]{1,0:T(8,128)} %lat_h.1, bf16[3,256,512]{2,1,0:T(8,128)(2,1)} %bitcast.3, s32[2,2,256]{2,1,0:T(2,128)} %bitcast.5, bf16[8,2048]{1,0:T(8,128)(2,1)} %bitcast.4, bf16[1,2048,2048]{2,1,0:T(8,128)(2,1)} %up_h.1, bf16[1,2048,2048]{2,1,0:T(8,128)(2,1)} %down_h.1), custom_call_target="tpu_custom_call" | custom-call | tf_op jit(solution)/shard_map/pallas_call | solution.py:457
  134.7 1.9 %copy.9 = f32[256,512]{1,0:T(8,128)} copy(f32[256,512]{1,0:T(8,128)} %shard_map.73) | data formatting | bytes 1048576

commit v2 on v1

--- a/solution.py
+++ b/solution.py
@@ -31,18 +31,19 @@
 
 
 def process_order(n_ep):
-    return list(range(n_ep))
+    return [4, 2, 5, 3, 6, 1] + list(range(7, n_ep)) + [0]
 
 
 def send_order(n_ep):
-    return list(range(n_ep))
+    return [0, 1, 2, 4, 3] + list(range(5, n_ep))
 
 
 SCHEDULE = (
-    "A0", "A1", "A2", "A3", "R0", "R1", "L", "W0", "W1", "F0", "A4", "R2", "G0.0", "A5", "R3", "G0.1", "G0.2",
-    "A6", "R4", "G0.3", "W2", "W3", "F1", "A7", "R5", "G1.0", "R6", "G1.1", "G1.2", "R7", "G1.3", "W4", "W5",
-    "F2", "S0", "S1", "G2.0", "G2.1", "G2.2", "G2.3", "W6", "W7", "F3", "S2", "S3", "M0", "M1", "G3.0",
-    "G3.1", "G3.2", "G3.3", "S4", "S5", "M2", "M3", "S6", "S7", "M4", "M5", "M6", "M7",
+    "X0", "X1", "A7", "A5", "A1", "R7", "A0", "R5", "L", "R1", "A3", "T", "R0", "W1", "W0", "F0.0", "A2",
+    "R3", "F0.1", "A4", "R2", "G0.0", "G0.1", "A6", "G0.2", "G0.3", "W3", "W2", "F1.0", "R4", "F1.1", "R6",
+    "G1.0", "G1.1", "S0", "G1.2", "S1", "G1.3", "W5", "W4", "F2.0", "F2.1", "G2.0", "G2.1", "S2", "G2.2",
+    "S3", "G2.3", "W7", "W6", "F3.0", "F3.1", "G3.0", "G3.1", "S4", "G3.2", "S5", "G3.3", "M0", "M1", "M2",
+    "M3", "S6", "S7", "M4", "M5", "M7", "M6",
 )
 
 
@@ -69,9 +70,10 @@
     cb = n_ep // nb
     jg, bg = n_ep // GROUPS, nb // GROUPS
     group_rows = jg * cap
-    nt = min(1024, ff)
+    nt = ff // 2
     order = process_order(n_ep)
     place = {mask: j for j, mask in enumerate(order)}
+    held = send_order(n_ep)[6:]
 
     def local(src, dst, i):
         copy = pltpu.make_async_copy(src, dst, wsem.at[i])
@@ -154,41 +156,15 @@
     share_one(ma_s, ma_r, ma_ss, ma_rs)
     share_one(mb_s, mb_r, mb_ss, mb_rs)
 
-    sent = []
-
-    def substep(sub, carry):
-        pending = []
-
-        def send(src, dst, ss, rs, to):
-            copy = remote(src, dst, ss, rs, to)
-            copy.start()
-            pending.append(copy)
-
-        def share(src, dst, ss, rs):
-            for dt in range(1, n_tp):
-                send(src.at[sub], dst.at[sub, dt - 1], ss.at[sub, dt - 1], rs.at[sub, dt - 1], peer_t(dt))
-
-        def shared(src, dst, ss, rs):
-            total = src[sub]
-            for dt in range(1, n_tp):
-                arrived(dst.at[sub, dt - 1], ss.at[sub, dt - 1], rs.at[sub, dt - 1], peer_t(dt))
-                total = total + dst[sub, dt - 1]
-            return total
-
-        current = cur_v[...]
-        sums = jnp.sum(current, axis=1, keepdims=True)
-        squares = jnp.sum(current * current, axis=1, keepdims=True)
-        lane = lax.broadcasted_iota(jnp.int32, (rows_t, 128), 1)
-        both = jnp.where(lane == 0, sums, jnp.where(lane == 1, squares, 0.0))
-        st_s[sub] = both.T[0:8]
-        share(st_s, st_r, st_ss, st_rs)
-
+    def found(s):
         spot = lax.broadcasted_iota(jnp.int32, (n_ep, rows_t), 0)
         experts = jnp.zeros((n_ep, rows_t), jnp.int32)
         for j in range(n_ep):
             experts = jnp.where(spot == j, xor_of(me_e, order[j], n_ep), experts)
-        routes = [rt_v[sub, k : k + 1, :] for k in range(2)]
-        hot = [routes[k] == experts for k in range(2)]
+        return [rt_v[s, k : k + 1, :] == experts for k in range(2)]
+
+    def tables(s):
+        hot = found(s)
         either = jnp.where(hot[0], 1.0, jnp.where(hot[1], 1.0, 0.0))
         earlier = lax.broadcasted_iota(jnp.int32, (rows_t, rows_t), 0) < lax.broadcasted_iota(
             jnp.int32, (rows_t, rows_t), 1
@@ -198,11 +174,45 @@
         slot = jnp.where(either > 0.5, slot, -1.0)
         ranks = lax.broadcasted_iota(jnp.int32, (cap, rows_t), 0).astype(F32)
         for j in range(n_ep):
-            disp_v[j] = jnp.where(slot[j : j + 1] == ranks, 1.0, 0.0).astype(BF)
+            disp_v[s, j] = jnp.where(slot[j : j + 1] == ranks, 1.0, 0.0).astype(BF)
         slot_t = turned(slot)
         ranks = lax.broadcasted_iota(jnp.int32, (rows_t, cap), 1).astype(F32)
         for j in range(n_ep):
-            pick_v[j] = jnp.where(slot_t[:, j : j + 1] == ranks, 1.0, 0.0).astype(BF)
+            pick_v[s, j] = jnp.where(slot_t[:, j : j + 1] == ranks, 1.0, 0.0).astype(BF)
+
+
+    sent = []
+
+    def substep(sub, carry):
+        pending = []
+
+        def send(src, dst, ss, rs, to):
+            copy = remote(src, dst, ss, rs, to)
+            copy.start()
+            pending.append(copy)
+
+        def share(src, dst, ss, rs):
+            for dt in range(1, n_tp):
+                send(src.at[sub], dst.at[sub, dt - 1], ss.at[sub, dt - 1], rs.at[sub, dt - 1], peer_t(dt))
+
+        def shared(src, dst, ss, rs):
+            total = src[sub]
+            for dt in range(1, n_tp):
+                arrived(dst.at[sub, dt - 1], ss.at[sub, dt - 1], rs.at[sub, dt - 1], peer_t(dt))
+                total = total + dst[sub, dt - 1]
+            return total
+
+        current = cur_v[...]
+        sums = jnp.sum(current, axis=1, keepdims=True)
+        squares = jnp.sum(current * current, axis=1, keepdims=True)
+        lane = lax.broadcasted_iota(jnp.int32, (rows_t, 128), 1)
+        both = jnp.where(lane == 0, sums, jnp.where(lane == 1, squares, 0.0))
+        st_s[sub] = both.T[0:8]
+        share(st_s, st_r, st_ss, st_rs)
+
+        @pl.when(sub == 0)
+        def _():
+            tables(0)
 
         @pl.when(sub == 0)
         def _():
@@ -214,17 +224,25 @@
         row_var = stats[:, 1:2] / model - row_mean * row_mean
         normed = (cur_v[...] - row_mean) * lax.rsqrt(row_var + 1e-06)
         mdl[...] = (normed * (1.0 + modv[sub, 1:2]) + modv[sub, 0:1]).astype(BF)
+        def dispatch(j):
+            send(out_b.at[sub, j], xb.at[sub, me_t, j], aa_ss.at[sub, j], aa_rs.at[sub, j], peer_e(j))
+
         for mask in send_order(n_ep):
             j = place[mask]
-            outgoing = jnp.dot(disp_v[j], mdl[...], preferred_element_type=F32).astype(BF)
+            outgoing = jnp.dot(disp_v[sub, j], mdl[...], preferred_element_type=F32).astype(BF)
             if mask == 0:
                 xb[sub, me_t, j] = outgoing
             else:
                 out_b[sub, j] = outgoing
-                send(out_b.at[sub, j], xb.at[sub, me_t, j], aa_ss.at[sub, j], aa_rs.at[sub, j], peer_e(j))
+                if mask not in held:
+                    dispatch(j)
         lg_s[sub] = lax.dot_general(rw_v[...], mdl[...], (((1,), (1,)), ((), ())), preferred_element_type=F32)
         share(lg_s, lg_r, lg_ss, lg_rs)
         mix_v[...] = jnp.zeros((rows_t, width), F32)
+
+        def step_x(i):
+            for mask in held[i * len(held) // 2 : (i + 1) * len(held) // 2]:
+                dispatch(place[mask])
 
         def step_a(b):
             js = pl.ds(b * cb, cb)
@@ -252,6 +270,8 @@
         def step_l():
             logits = shared(lg_s, lg_r, lg_ss, lg_rs)
             ids = lax.broadcasted_iota(jnp.int32, (n_ep, rows_t), 0)
+            routes = [rt_v[sub, k : k + 1, :] for k in range(2)]
+            hot = found(sub)
             probs = [
                 jax.nn.sigmoid(jnp.sum(jnp.where(routes[k] == ids, logits, 0.0), axis=0, keepdims=True))
                 for k in range(2)
@@ -260,24 +280,20 @@
             gates = jnp.where(hot[0], probs[0] / both_p, jnp.where(hot[1], probs[1] / both_p, 0.0))
             gate_v[...] = turned(gates)
 
-        def first_gemm(g):
-            if g == 0:
+        def first_gemm(g, part):
+            if g == 0 and part == 0:
 
                 @pl.when(sub == 0)
                 def _():
                     up_c.wait()
 
-            def body(n, carry):
-                at = pl.ds(pl.multiple_of(n * nt, nt), nt)
-                total = None
-                for t in range(n_tp):
-                    rows = xb[sub, t, pl.ds(g * jg, jg)].reshape(group_rows, width)
-                    term = jnp.dot(rows, up_v[pl.ds(t * width, width), at], preferred_element_type=F32)
-                    total = term if total is None else total + term
-                hid[:, at] = jax.nn.gelu(total).astype(BF)
-                return carry
-
-            lax.fori_loop(0, ff // nt, body, 0)
+            at = pl.ds(part * nt, nt)
+            total = None
+            for t in range(n_tp):
+                rows = xb[sub, t, pl.ds(g * jg, jg)].reshape(group_rows, width)
+                term = jnp.dot(rows, up_v[pl.ds(t * width, width), at], preferred_element_type=F32)
+                total = term if total is None else total + term
+            hid[:, at] = jax.nn.gelu(total).astype(BF)
 
         def slice_dot(t, store):
             sw = min(512, width)
@@ -355,17 +371,18 @@
                     came = ret_r[sub, j]
                 else:
                     came = ret_s[sub, j]
-                mix_v[...] += gate_v[:, j : j + 1] * jnp.dot(pick_v[j], came, preferred_element_type=F32)
-
-        steps = dict(A=step_a, R=step_r, W=step_w, F=first_gemm, S=send_back, M=mix_in)
+                mix_v[...] += gate_v[:, j : j + 1] * jnp.dot(pick_v[sub, j], came, preferred_element_type=F32)
+
+        def step_t():
+            @pl.when(sub == 0)
+            def _():
+                tables(1)
+
+        steps = dict(
+            X=step_x, A=step_a, R=step_r, W=step_w, L=step_l, T=step_t, F=first_gemm, G=second_gemm, S=send_back, M=mix_in
+        )
         for word in SCHEDULE:
-            if word == "L":
-                step_l()
-            elif word[0] == "G":
-                g, part = word[1:].split(".")
-                second_gemm(int(g), int(part))
-            else:
-                steps[word[0]](int(word[1:]))
+            steps[word[0]](*[int(n) for n in word[1:].split(".") if n])
 
         @pl.when(sub == 0)
         def _():
@@ -428,8 +445,8 @@
         vm((2, experts, tok_rows), F32),
         vm((2, n_tp - 1, experts, tok_rows), F32),
         vm((tok_rows, width), BF),
-        vm((n_ep, cap, tok_rows), BF),
-        vm((n_ep, tok_rows, cap), BF),
+        vm((2, n_ep, cap, tok_rows), BF),
+        vm((2, n_ep, tok_rows, cap), BF),
         vm((tok_rows, 128), F32),
         vm((tok_rows, width), F32),
         vm((2, n_ep, cap, width), BF),

time: 137 us -> 122 us (0.89)
  the two profiles are of different devices: /device:TPU:17 before, /device:TPU:0 now
where the time goes in v2:
time: 122 us; the launch traced here: 120 us
  Pallas kernels  118 us (97%)
  local copies, waits for them, and re-layouts  1.87 us (2%)
    pallas_call x1, Pallas kernels, per_device(): pl.pallas_call(functools.partial(kernel, n_ep, n_tp), out_shape=jax.Shape...  118 us

profile of v2, /device:TPU:0, one launch (start us, length us, event | category | flops | bytes accessed | tf_op | source)
XLA Modules:
  0.0 119.5 jit_solution(12852203898290034621)
XLA Ops:
  0.0 117.7 %shard_map.73 = f32[256,512]{1,0:T(8,128)} custom-call(s32[3]{0:T(128)} %ts.1, f32[256,512]{1,0:T(8,128)} %lat_h.1, bf16[3,256,512]{2,1,0:T(8,128)(2,1)} %bitcast.3, s32[2,2,256]{2,1,0:T(2,128)} %bitcast.5, bf16[8,2048]{1,0:T(8,128)(2,1)} %bitcast.4, bf16[1,2048,2048]{2,1,0:T(8,128)(2,1)} %up_h.1, bf16[1,2048,2048]{2,1,0:T(8,128)(2,1)} %down_h.1), custom_call_target="tpu_custom_call" | custom-call | tf_op jit(solution)/shard_map/pallas_call | solution.py:474
  117.7 1.9 %copy.9 = f32[256,512]{1,0:T(8,128)} copy(f32[256,512]{1,0:T(8,128)} %shard_map.73) | data formatting | bytes 1048576

commit v3 on v2

--- a/solution.py
+++ b/solution.py
@@ -35,14 +35,14 @@
 
 
 def send_order(n_ep):
-    return [0, 1, 2, 4, 3] + list(range(5, n_ep))
+    return [0, 1, 2, 4, 5, 3] + list(range(6, n_ep))
 
 
 SCHEDULE = (
     "X0", "X1", "A7", "A5", "A1", "R7", "A0", "R5", "L", "R1", "A3", "T", "R0", "W1", "W0", "F0.0", "A2",
-    "R3", "F0.1", "A4", "R2", "G0.0", "G0.1", "A6", "G0.2", "G0.3", "W3", "W2", "F1.0", "R4", "F1.1", "R6",
-    "G1.0", "G1.1", "S0", "G1.2", "S1", "G1.3", "W5", "W4", "F2.0", "F2.1", "G2.0", "G2.1", "S2", "G2.2",
-    "S3", "G2.3", "W7", "W6", "F3.0", "F3.1", "G3.0", "G3.1", "S4", "G3.2", "S5", "G3.3", "M0", "M1", "M2",
+    "R3", "F0.1", "A4", "G0.0", "A6", "G0.1", "R2", "G0.2", "G0.3", "W3", "W2", "F1.0", "R4", "F1.1", "R6",
+    "G1.0", "G1.1", "G1.2", "S0", "S1", "G1.3", "W5", "W4", "F2.0", "F2.1", "G2.0", "G2.1", "G2.2", "S2",
+    "S3", "G2.3", "W7", "W6", "F3.0", "F3.1", "G3.0", "G3.1", "G3.2", "S4", "S5", "G3.3", "M0", "M1", "M2",
     "M3", "S6", "S7", "M4", "M5", "M7", "M6",
 )
 

time: 122 us -> 118 us (0.967); the launches traced: 120 us -> 118 us
  Pallas kernels: 118 us -> 116 us
    pallas_call x1, Pallas kernels: 118 us -> 116 us  [per_device(): pl.pallas_call(functools.partial(kernel, n_ep, n_tp), out_shape=jax.Shape...]
where the time goes in v3:
time: 118 us
  Pallas kernels  116 us (98%)
  local copies, waits for them, and re-layouts  1.87 us (2%)
    pallas_call x1, Pallas kernels, per_device(): pl.pallas_call(functools.partial(kernel, n_ep, n_tp), out_shape=jax.Shape...  116 us

profile of v3, /device:TPU:0, one launch (start us, length us, event | category | flops | bytes accessed | tf_op | source)
XLA Modules:
  0.0 117.7 jit_solution(4086510948123864578)
XLA Ops:
  0.0 115.8 %shard_map.73 = f32[256,512]{1,0:T(8,128)} custom-call(s32[3]{0:T(128)} %ts.1, f32[256,512]{1,0:T(8,128)} %lat_h.1, bf16[3,256,512]{2,1,0:T(8,128)(2,1)} %bitcast.3, s32[2,2,256]{2,1,0:T(2,128)} %bitcast.5, bf16[8,2048]{1,0:T(8,128)(2,1)} %bitcast.4, bf16[1,2048,2048]{2,1,0:T(8,128)(2,1)} %up_h.1, bf16[1,2048,2048]{2,1,0:T(8,128)(2,1)} %down_h.1), custom_call_target="tpu_custom_call" | custom-call | tf_op jit(solution)/shard_map/pallas_call | solution.py:474
  115.8 1.9 %copy.9 = f32[256,512]{1,0:T(8,128)} copy(f32[256,512]{1,0:T(8,128)} %shard_map.73) | data formatting | bytes 1048576
